TPU v7x, 32 devices: a whole 2x2x4 slice. The times are simulated.
32 devices in a mesh: rep: 4 (over x, core), shard: 8 (over z, y).
Axes of the slice: x: 2, y: 2, z: 4, core: 2. Of those that a mesh axis runs over, the one named last changes fastest.
Arguments:
- images: bfloat16 [32, 256, 1152], P(('rep', 'shard')), may hold values from -6 to 6
- cotangent: bfloat16 [32, 256, 1152], P(('rep', 'shard')), may hold values from -6 to 6
- w_qkv: bfloat16 [1152, 3456], P('shard'), may hold values from -2 to 2
- w_out: bfloat16 [1152, 1152], P('shard'), may hold values from -0.75 to 0.75
- w_up: bfloat16 [1152, 4304], P('shard'), may hold values from -0.1875 to 0.1875
- w_down: bfloat16 [1152, 4304], P('shard'), may hold values from -0.125 to 0.125
- vectors: bfloat16 [1152, 8], P('shard'), may hold values from -3 to 3, as said below
- up_bias: bfloat16 [4304], replicated, may hold values from -3 to 3
Outputs:
- outputs: bfloat16 [32, 256, 1152], P(('rep', 'shard'))
- input_grad: bfloat16 [32, 256, 1152], P(('rep', 'shard'))
- qkv_grad: float32 [1152, 3456], P('shard')
- out_grad: float32 [1152, 1152], P('shard')
- up_grad: float32 [1152, 4304], P('shard')
- down_grad: float32 [1152, 4304], P('shard')
- vectors_grad: float32 [1152, 8], P('shard')
- up_bias_grad: float32 [4304], replicated
Inputs may be any that keep to these rules, and one draw needn't show every extreme that they name: `vectors`: columns 0 and 5 (the norms' gains) are positive; the other columns have either sign.
All inputs are finite; a program needn't handle non-finite values.
Results may differ from a plain program's by a relative error of at most 0.014.
Values may be sent and summed in bfloat16 or wider, within the bound.
A program may use at most 256 MiB of HBM per device.

v0:
```python
import math
import jax
import jax.numpy as jnp
from jax import lax
from jax.sharding import PartitionSpec as P

HEAD_DIM = 72
EPSILON = 1e-06
GELU_COEF = 0.044715
ROOT_TWO_PI = math.sqrt(2.0 / math.pi)


def batched(pattern, left_op, right_op):
    return jnp.einsum(pattern, left_op, right_op, preferred_element_type=jnp.float32)


def contract_rows(left_op, right_op):
    return lax.dot_general(
        left_op, right_op, (((0,), (0,)), ((), ())), preferred_element_type=jnp.float32
    )


def contract_cols(left_op, right_op):
    return lax.dot_general(
        left_op, right_op, (((1,), (1,)), ((), ())), preferred_element_type=jnp.float32
    )


def norm_rows(hidden):
    row_mean = jnp.mean(hidden, axis=-1, keepdims=True)
    centered = hidden - row_mean
    variance = jnp.mean(centered * centered, axis=-1, keepdims=True)
    inv_std = lax.rsqrt(variance + EPSILON)
    return (centered * inv_std, inv_std)


def norm_back(grad_normed, normed, inv_std):
    mean_grad = jnp.mean(grad_normed, axis=-1, keepdims=True)
    mean_proj = jnp.mean(grad_normed * normed, axis=-1, keepdims=True)
    return inv_std * (grad_normed - mean_grad - normed * mean_proj)


def gelu_parts(pre_act):
    tanh_term = jnp.tanh(ROOT_TWO_PI * (pre_act + GELU_COEF * pre_act * pre_act * pre_act))
    activated = 0.5 * pre_act * (1.0 + tanh_term)
    derivative = 0.5 * (1.0 + tanh_term) + 0.5 * pre_act * (
        1.0 - tanh_term * tanh_term
    ) * ROOT_TWO_PI * (1.0 + 3.0 * GELU_COEF * pre_act * pre_act)
    return (activated, derivative)


def split_heads(tensor, batch_count, seq_len, head_size):
    return tensor.reshape(batch_count, seq_len, tensor.shape[-1] // head_size, head_size)


def forward_pass(images, w_qkv, w_out, w_up, w_down, vectors, up_bias):
    params = vectors.astype(jnp.float32)
    batch_count, seq_len, model_width = images.shape
    flat_rows = images.reshape(batch_count * seq_len, model_width).astype(jnp.float32)
    normed_one, inv_one = norm_rows(flat_rows)
    input_one = (normed_one * params[:, 0] + params[:, 1]).astype(jnp.bfloat16)
    projected = jnp.dot(input_one, w_qkv, preferred_element_type=jnp.float32)
    query = (projected[:, :model_width] + params[:, 2]).astype(jnp.bfloat16)
    keys_all = projected[:, model_width : 2 * model_width].astype(jnp.bfloat16)
    values_all = (projected[:, 2 * model_width :] + params[:, 3]).astype(jnp.bfloat16)
    score_scale = 1.0 / math.sqrt(HEAD_DIM)
    query_heads = split_heads(query, batch_count, seq_len, HEAD_DIM)
    key_heads = split_heads(keys_all, batch_count, seq_len, HEAD_DIM)
    value_heads = split_heads(values_all, batch_count, seq_len, HEAD_DIM)
    scores = batched("bqhd,bkhd->bhqk", query_heads, key_heads) * score_scale
    row_max = jnp.max(scores, axis=-1, keepdims=True)
    exponent = jnp.exp(scores - row_max)
    row_total = jnp.sum(exponent, axis=-1, keepdims=True)
    weights = (exponent / row_total).astype(jnp.bfloat16)
    logsum = row_max + jnp.log(row_total)
    attended = (
        batched("bhqk,bkhd->bqhd", weights, value_heads)
        .reshape(batch_count * seq_len, model_width)
        .astype(jnp.bfloat16)
    )
    middle = flat_rows + jnp.dot(attended, w_out, preferred_element_type=jnp.float32) + params[:, 4]
    normed_two, inv_two = norm_rows(middle)
    input_two = (normed_two * params[:, 5] + params[:, 6]).astype(jnp.bfloat16)
    pre_act = jnp.dot(input_two, w_up, preferred_element_type=jnp.float32) + up_bias.astype(
        jnp.float32
    )
    activated, derivative = gelu_parts(pre_act)
    act_bf = activated.astype(jnp.bfloat16)
    final = middle + contract_cols(act_bf, w_down) + params[:, 7]
    outputs = final.astype(jnp.bfloat16).reshape(batch_count, seq_len, model_width)
    saved = (
        normed_one,
        inv_one,
        input_one,
        query,
        keys_all,
        values_all,
        logsum,
        attended,
        normed_two,
        inv_two,
        input_two,
        derivative,
        act_bf,
    )
    return (outputs, saved)


def backward_pass(cotangent, saved, w_qkv, w_out, w_up, w_down, vectors):
    (
        normed_one,
        inv_one,
        input_one,
        query,
        keys_all,
        values_all,
        logsum,
        attended,
        normed_two,
        inv_two,
        input_two,
        derivative,
        act_bf,
    ) = saved
    params = vectors.astype(jnp.float32)
    batch_count, seq_len, model_width = cotangent.shape
    grad_bf = cotangent.reshape(batch_count * seq_len, model_width)
    grad_final = grad_bf.astype(jnp.float32)
    down_term = contract_rows(grad_bf, act_bf)
    grad_act = jnp.dot(grad_bf, w_down, preferred_element_type=jnp.float32)
    grad_pre = grad_act * derivative
    upb_term = jnp.sum(grad_pre, axis=0)
    grad_pre_bf = grad_pre.astype(jnp.bfloat16)
    up_term = contract_rows(input_two, grad_pre_bf)
    grad_two = contract_cols(grad_pre_bf, w_up)
    grad_gain_two = jnp.sum(grad_two * normed_two, axis=0)
    grad_bias_two = jnp.sum(grad_two, axis=0)
    grad_middle = grad_final + norm_back(grad_two * params[:, 5], normed_two, inv_two)
    grad_out_bias = jnp.sum(grad_middle, axis=0)
    grad_middle_bf = grad_middle.astype(jnp.bfloat16)
    out_term = contract_rows(attended, grad_middle_bf)
    grad_att = contract_cols(grad_middle_bf, w_out).astype(jnp.bfloat16)
    score_scale = 1.0 / math.sqrt(HEAD_DIM)
    query_heads = split_heads(query, batch_count, seq_len, HEAD_DIM)
    key_heads = split_heads(keys_all, batch_count, seq_len, HEAD_DIM)
    value_heads = split_heads(values_all, batch_count, seq_len, HEAD_DIM)
    grad_heads = split_heads(grad_att, batch_count, seq_len, HEAD_DIM)
    scores = batched("bqhd,bkhd->bhqk", query_heads, key_heads) * score_scale
    probs = jnp.exp(scores - logsum)
    probs_bf = probs.astype(jnp.bfloat16)
    grad_value = batched("bhqk,bqhd->bkhd", probs_bf, grad_heads)
    grad_prob = batched("bqhd,bkhd->bhqk", grad_heads, value_heads)
    delta = jnp.sum(probs * grad_prob, axis=-1, keepdims=True)
    grad_score = (probs * (grad_prob - delta) * score_scale).astype(jnp.bfloat16)
    grad_query = batched("bhqk,bkhd->bqhd", grad_score, key_heads)
    grad_key = batched("bhqk,bqhd->bkhd", grad_score, query_heads)
    flat_count = batch_count * seq_len
    grad_query = grad_query.reshape(flat_count, model_width)
    grad_key = grad_key.reshape(flat_count, model_width)
    grad_value = grad_value.reshape(flat_count, model_width)
    grad_qbias = jnp.sum(grad_query, axis=0)
    grad_vbias = jnp.sum(grad_value, axis=0)
    grad_proj = jnp.concatenate([grad_query, grad_key, grad_value], axis=1).astype(jnp.bfloat16)
    qkv_term = contract_rows(input_one, grad_proj)
    grad_one = contract_cols(grad_proj, w_qkv)
    grad_gain_one = jnp.sum(grad_one * normed_one, axis=0)
    grad_bias_one = jnp.sum(grad_one, axis=0)
    grad_input = grad_middle + norm_back(grad_one * params[:, 0], normed_one, inv_one)
    grad_down_bias = jnp.sum(grad_final, axis=0)
    vector_term = jnp.stack(
        [
            grad_gain_one,
            grad_bias_one,
            grad_qbias,
            grad_vbias,
            grad_out_bias,
            grad_gain_two,
            grad_bias_two,
            grad_down_bias,
        ],
        axis=1,
    )
    input_grad = grad_input.astype(jnp.bfloat16).reshape(batch_count, seq_len, model_width)
    return (input_grad, (qkv_term, out_term, up_term, down_term, vector_term), upb_term)


def per_device(images, cotangent, w_qkv, w_out, w_up, w_down, vectors, up_bias):
    whole = (
        lax.all_gather(w_qkv, "shard", axis=0, tiled=True),
        lax.all_gather(w_out, "shard", axis=0, tiled=True),
        lax.all_gather(w_up, "shard", axis=0, tiled=True),
        lax.all_gather(w_down, "shard", axis=0, tiled=True),
        lax.all_gather(vectors, "shard", axis=0, tiled=True),
    )
    outputs, saved = forward_pass(images, whole[0], whole[1], whole[2], whole[3], whole[4], up_bias)
    again = (
        lax.all_gather(w_qkv, "shard", axis=0, tiled=True),
        lax.all_gather(w_out, "shard", axis=0, tiled=True),
        lax.all_gather(w_up, "shard", axis=0, tiled=True),
        lax.all_gather(w_down, "shard", axis=0, tiled=True),
        lax.all_gather(vectors, "shard", axis=0, tiled=True),
    )
    input_grad, terms, upb_term = backward_pass(
        cotangent, saved, again[0], again[1], again[2], again[3], again[4]
    )
    upb_total = lax.psum(upb_term, ("rep", "shard"))
    owned = (
        lax.psum_scatter(terms[0], "shard", scatter_dimension=0, tiled=True),
        lax.psum_scatter(terms[1], "shard", scatter_dimension=0, tiled=True),
        lax.psum_scatter(terms[2], "shard", scatter_dimension=0, tiled=True),
        lax.psum_scatter(terms[3], "shard", scatter_dimension=0, tiled=True),
        lax.psum_scatter(terms[4], "shard", scatter_dimension=0, tiled=True),
    )
    parted = (
        lax.psum_scatter(owned[0], "rep", scatter_dimension=0, tiled=True),
        lax.psum_scatter(owned[1], "rep", scatter_dimension=0, tiled=True),
        lax.psum_scatter(owned[2], "rep", scatter_dimension=0, tiled=True),
        lax.psum_scatter(owned[3], "rep", scatter_dimension=0, tiled=True),
        lax.psum_scatter(owned[4], "rep", scatter_dimension=0, tiled=True),
    )
    summed = (
        lax.all_gather(parted[0], "rep", axis=0, tiled=True),
        lax.all_gather(parted[1], "rep", axis=0, tiled=True),
        lax.all_gather(parted[2], "rep", axis=0, tiled=True),
        lax.all_gather(parted[3], "rep", axis=0, tiled=True),
        lax.all_gather(parted[4], "rep", axis=0, tiled=True),
    )
    return (outputs, input_grad, summed[0], summed[1], summed[2], summed[3], summed[4], upb_total)


def solution(mesh):
    placed = (
        P(("rep", "shard"), None, None),
        P(("rep", "shard"), None, None),
        P("shard", None),
        P("shard", None),
        P("shard", None),
        P("shard", None),
        P("shard", None),
        P(),
    )
    return jax.shard_map(
        per_device,
        mesh=mesh,
        in_specs=placed,
        out_specs=(
            P(("rep", "shard"), None, None),
            P(("rep", "shard"), None, None),
            P("shard", None),
            P("shard", None),
            P("shard", None),
            P("shard", None),
            P("shard", None),
            P(),
        ),
        check_vma=False,
    )
```

profile of v0, /device:TPU:0, one launch (start us, length us, event | category | flops | bytes accessed | tf_op | source)
XLA Modules:
  0.0 1816.3 jit_solution(12791949931599254159)
XLA Ops:
  10.0 33.4 %all-gather = bf16[8,144,8]{1,2,0:T(8,128)(2,1)S(1)} all-gather(bf16[1,144,8]{1,2,0:T(8,128)(2,1)S(1)} %bitcast.145), channel_id=1, replica_groups=mesh['rep'=4,'shard'=8] {'shard'}, dimensions={0}, use_global_device_ids=true | all-gather | bytes 20736 | tf_op jit(solution)/shard_map/all_gather | solution.py:193
  45.3 86.9 %all-gather.14.cloned.1.call-done = bf16[1152,3456]{1,0:T(8,128)(2,1)} async-done(((bf16[144,3456]{1,0:T(8,128)(2,1)}), bf16[1152,3456]{1,0:T(8,128)(2,1)}) %all-gather.14.cloned.1.call-update) | async-done | bytes 7962640 | tf_op jit(solution)/shard_map/all_gather | solution.py:189
  143.0 44.5 %all-gather.16.cloned.1.call-done = bf16[1152,1152]{1,0:T(8,128)(2,1)} async-done(((bf16[144,1152]{1,0:T(8,128)(2,1)}), bf16[1152,1152]{1,0:T(8,128)(2,1)}) %all-gather.16.cloned.1.call-update) | async-done | bytes 2654224 | tf_op jit(solution)/shard_map/all_gather | solution.py:190
  190.8 142.4 %all-gather.18.cloned.1.call-done = bf16[1152,4304]{1,0:T(8,128)(2,1)} async-done(((bf16[144,4304]{1,0:T(8,128)(2,1)}), bf16[1152,4304]{1,0:T(8,128)(2,1)}) %all-gather.18.cloned.1.call-update) | async-done | bytes 9916432 | tf_op jit(solution)/shard_map/all_gather | solution.py:191
  333.2 8.3 convolution_add_fusion
  343.5 8.7 convolution_bitcast_fusion
  352.2 21.6 %copy.63 = f32[1152,4304]{1,0:T(8,128)} copy(f32[1152,4304]{0,1:T(8,128)} %convolution_bitcast_fusion) | data formatting | bytes 39665664
  373.9 104.3 %all-gather.20.cloned.1.call-done = bf16[1152,4304]{1,0:T(8,128)(2,1)} async-done(((bf16[144,4304]{1,0:T(8,128)(2,1)}), bf16[1152,4304]{1,0:T(8,128)(2,1)}) %all-gather.20.cloned.1.call-update) | async-done | bytes 9916432 | tf_op jit(solution)/shard_map/all_gather | solution.py:192
  478.2 10.5 fusion.98
  488.8 8.7 multiply_reduce_fusion.2
  512.7 9.1 fusion.51
  521.7 10.1 fusion.93
  545.7 11.5 fusion.65
  559.1 252.7 %reduce-scatter.24.cloned.1.call-done = f32[144,4304]{1,0:T(8,128)} async-done(((f32[1152,4304]{1,0:T(8,128)}), f32[144,4304]{1,0:T(8,128)}) %reduce-scatter.24.cloned.1.call-update) | async-done | bytes 2479120
  816.7 102.1 %reduce-scatter.20.cloned.1.call-done = f32[144,1152]{1,0:T(8,128)} async-done(((f32[1152,1152]{1,0:T(8,128)}), f32[144,1152]{1,0:T(8,128)}) %reduce-scatter.20.cloned.1.call-update) | async-done | bytes 663568 | tf_op jit(solution)/shard_map/reduce_scatter | solution.py:209
  918.8 271.9 %reduce-scatter.18.cloned.1.call-done = f32[144,3456]{1,0:T(8,128)} async-done(((f32[1152,3456]{1,0:T(8,128)}), f32[144,3456]{1,0:T(8,128)}) %reduce-scatter.18.cloned.1.call-update) | async-done | bytes 1990672 | tf_op jit(solution)/shard_map/reduce_scatter | solution.py:208
  1190.7 334.6 %reduce-scatter.22.cloned.1.call-done = f32[144,4304]{1,0:T(8,128)} async-done(((f32[1152,4304]{1,0:T(8,128)}), f32[144,4304]{1,0:T(8,128)}) %reduce-scatter.22.cloned.1.call-update) | async-done | bytes 2479120 | tf_op jit(solution)/shard_map/reduce_scatter | solution.py:210
  1525.3 103.3 %fusion.90 = (f32[48,3456]{1,0:T(8,128)}, f32[48,1152]{1,0:T(8,128)}, f32[40,4304]{1,0:T(8,128)}) fusion(f32[144,3456]{1,0:T(8,128)} %reduce-scatter.18.cloned.1.call-done, f32[144,1152]{1,0:T(8,128)} %reduce-scatter.20.cloned.1.call-done, f32[144,4304]{1,0:T(8,128)} %reduce-scatter.22.cloned.1.call-done), kind=kCustom, calls=%all-reduce-scatter.3 | all-reduce-scatter fusion | flops 1573378 | bytes 6707200
  1656.9 8.6 collective-permute-start.2
  1682.4 9.5 fusion.23
  1699.9 39.3 %psum.7 = f32[4304]{0:T(1024)} all-reduce(f32[4304]{0:T(1024)S(1)} %copy-done.34), channel_id=1, replica_groups=mesh['rep'=4,'shard'=8] {'rep','shard'}, use_global_device_ids=true, to_apply=%region_30.0 | all-reduce | flops 4304 | bytes 34432 | tf_op jit(solution)/shard_map/psum | solution.py:206
  1753.5 10.2 all-gather.2
  1767.2 10.4 all-gather.24.cloned.1.call-done
  1780.6 25.7 %all-gather.26.cloned.1.call-done = f32[4,36,4304]{2,1,0:T(8,128)} async-done(((f32[1,36,4304]{2,1,0:T(8,128)}), f32[4,36,4304]{2,1,0:T(8,128)}) %all-gather.26.cloned.1.call-update) | async-done | bytes 2479120 | tf_op jit(solution)/shard_map/all_gather | solution.py:225
  (187 shorter events, 131.2 us)
Async XLA Ops:
  7.2 125.0 %all-gather.14.cloned.1.call-start = ((), (), s32[]{:S(2)}) async-start(), calls=%async_computation.5 | async-start | bytes 8957952 | tf_op jit(solution)/shard_map/all_gather | solution.py:189
  7.9 179.6 %all-gather.16.cloned.1.call-start = ((), (), s32[]{:S(2)}) async-start(), calls=%async_computation.6 | async-start | bytes 2985984 | tf_op jit(solution)/shard_map/all_gather | solution.py:190
  8.7 324.5 %all-gather.18.cloned.1.call-start = ((), (), s32[]{:S(2)}) async-start(), calls=%async_computation.7 | async-start | bytes 11280384 | tf_op jit(solution)/shard_map/all_gather | solution.py:191
  9.4 468.8 %all-gather.20.cloned.1.call-start = ((), (), s32[]{:S(2)}) async-start(), calls=%async_computation.8 | async-start | bytes 11280384 | tf_op jit(solution)/shard_map/all_gather | solution.py:192
  10.0 801.8 %reduce-scatter.24.cloned.1.call-start = ((), (), s32[]{:S(2)}) async-start(), calls=%async_computation.15 | async-start | bytes 22560768
  44.8 93.4 %copy-start.20 = (f32[1152]{0:T(1024)}, f32[1152]{0:T(1024)S(1)}, u32[]{:S(2)}) copy-start(f32[1152]{0:T(1024)S(1)} %get-tuple-element.22) | copy-start | bytes 13828
  187.6 145.6 %copy-start.18 = (f32[1152]{0:T(1024)S(1)}, f32[1152]{0:T(1024)}, u32[]{:S(2)}) copy-start(f32[1152]{0:T(1024)} %get-tuple-element.18) | copy-start | bytes 13828
  187.6 145.6 %copy-start.35 = (f32[4304]{0:T(1024)S(1)}, f32[4304]{0:T(1024)}, u32[]{:S(2)}) copy-start(f32[4304]{0:T(1024)} %convert_element_type.84) | copy-start | bytes 51652
  190.5 298.3 %copy-start.24 = (f32[256]{0:T(256)}, f32[256]{0:T(256)S(1)}, u32[]{:S(2)}) copy-start(f32[256]{0:T(256)S(1)} %broadcast_multiply_fusion.4) | copy-start | bytes 3076
  190.8 298.0 %copy-start.29 = (f32[256]{0:T(256)}, f32[256]{0:T(256)S(1)}, u32[]{:S(2)}) copy-start(f32[256]{0:T(256)S(1)} %add_rsqrt_fusion) | copy-start | bytes 3076
  373.9 544.9 %reduce-scatter.20.cloned.1.call-start = ((), (), s32[]{:S(2)}) async-start(), calls=%async_computation.10 | async-start | bytes 5971968 | tf_op jit(solution)/shard_map/reduce_scatter | solution.py:209
  502.6 688.1 %reduce-scatter.18.cloned.1.call-start = ((), (), s32[]{:S(2)}) async-start(), calls=%async_computation.9 | async-start | bytes 17915904 | tf_op jit(solution)/shard_map/reduce_scatter | solution.py:208
  545.0 980.4 %reduce-scatter.22.cloned.1.call-start = ((), (), s32[]{:S(2)}) async-start(), calls=%async_computation.11 | async-start | bytes 22560768 | tf_op jit(solution)/shard_map/reduce_scatter | solution.py:210
  557.2 1117.7 %all-reduce.11.cloned.1.call-start = ((), (), s32[]{:S(2)}) async-start(), calls=%async_computation.17 | async-start | bytes 8814592
  816.6 816.5 %copy-start.5 = (bf16[1,256,16,72]{1,3,2,0:T(8,128)(2,1)S(1)}, bf16[1,256,16,72]{1,3,2,0:T(8,128)(2,1)}, u32[]{:S(2)}) copy-start(bf16[1,256,16,72]{1,3,2,0:T(8,128)(2,1)} %copy-done.4) | copy-start | bytes 1769476
  816.6 816.5 %copy-start.28 = (f32[256]{0:T(256)S(1)}, f32[256]{0:T(256)}, u32[]{:S(2)}) copy-start(f32[256]{0:T(256)} %copy-done.26) | copy-start | bytes 3076
  816.7 816.5 %copy-start.33 = (f32[256]{0:T(256)S(1)}, f32[256]{0:T(256)}, u32[]{:S(2)}) copy-start(f32[256]{0:T(256)} %copy-done.31) | copy-start | bytes 3076
  816.7 922.5 %reduce-scatter.26.cloned.1.call-start = ((), (), s32[]{:S(2)}) async-start(), calls=%async_computation.16 | async-start | bytes 663552
  1630.5 16.3 collective-permute-start
  1646.8 117.8 %all-gather.22.cloned.1.call-start = ((), (), s32[]{:S(2)}) async-start(), calls=%async_computation.12 | async-start | bytes 2764800 | tf_op jit(solution)/shard_map/all_gather | solution.py:222
  1655.9 121.8 %all-gather.24.cloned.1.call-start = ((), (), s32[]{:S(2)}) async-start(), calls=%async_computation.13 | async-start | bytes 3481600 | tf_op jit(solution)/shard_map/all_gather | solution.py:224
  1656.9 9.8 collective-permute-start.2
  1673.8 132.5 %all-gather.26.cloned.1.call-start = ((), (), s32[]{:S(2)}) async-start(), calls=%async_computation.14 | async-start | bytes 3481600 | tf_op jit(solution)/shard_map/all_gather | solution.py:225
  1692.0 61.2 %collective-permute-start.1 = (f32[36,1152]{1,0:T(8,128)S(1)}, f32[36,1152]{1,0:T(8,128)S(1)}, u32[]{:S(2)}, u32[]{:S(2)}) collective-permute-start(f32[36,1152]{1,0:T(8,128)S(1)} %slice.59), channel_id=1, source_target_pairs={{0,8},{8,16},{16,24},{1,9},{9,17},{17,25},{2,10},{10,18},{18,26},{... | collective-permute-start | bytes 497672
  (35 other events, 464.5 us)
Sparse Core Ops, SparseCore 0:
  10.2 121.9 all-gather.13
  134.4 53.1 all-gather.15
  189.7 143.3 all-gather.17
  335.2 142.9 all-gather.19
  482.0 329.7 reduce-scatter.23
  815.2 103.5 reduce-scatter.19
  922.7 268.0 reduce-scatter.17
  1194.7 330.6 reduce-scatter.21
  1527.8 129.9 all-reduce.10
  1660.9 63.1 reduce-scatter.25
  1725.6 22.8 all-gather.21
  1749.9 27.6 all-gather.23
  1779.2 27.0 all-gather.25
where the time goes:
time: 1820 us
  waiting for transfers between devices  1380 us (76%)
  blocking collectives  198 us (11%)
  matrix products  118 us (6%)
  local copies, waits for them, and re-layouts  79 us (4%)
  starting transfers between devices  19.1 us (1%)
    reduce_scatter x1, waiting for transfers between devices, per_device(): lax.psum_scatter(terms[2], 'shard', scatter_dimension=0, tiled=True)  335 us
    reduce_scatter x1, waiting for transfers between devices, per_device(): lax.psum_scatter(terms[0], 'shard', scatter_dimension=0, tiled=True)  272 us
    unnamed x19, waiting for transfers between devices  256 us
    all_gather x1, waiting for transfers between devices, per_device(): lax.all_gather(w_up, 'shard', axis=0, tiled=True)  142 us
    unnamed x2, blocking collectives  110 us
    all_gather x1, waiting for transfers between devices, per_device(): lax.all_gather(w_down, 'shard', axis=0, tiled=True)  104 us
    reduce_scatter x1, waiting for transfers between devices, per_device(): lax.psum_scatter(terms[1], 'shard', scatter_dimension=0, tiled=True)  102 us
    all_gather x1, waiting for transfers between devices, per_device(): lax.all_gather(w_qkv, 'shard', axis=0, tiled=True)  86.9 us
  transfers between devices with their start and end apart: 16, of which 11 were waited for; matrix products, arithmetic and copies ran while one was open for 16% of the time, Pallas kernels for 0%

commit v1 on v0

--- a/solution.py
+++ b/solution.py
@@ -185,10 +185,39 @@
 
 
 def per_device(images, cotangent, w_qkv, w_out, w_up, w_down, vectors, up_bias):
+
+    def follow_ports(out_dim, m):
+        later = jax.lax.axis_size("shard")
+        piece_next = jax.lax.axis_index("shard")
+        current_block, val, outcome_arr = (later, piece_next, m.shape[out_dim])
+        in_order = []
+        for p in [*range(current_block)]:
+            in_order.append((p, (p + 1) % current_block))
+        by_rank = []
+        for p in tuple(range(current_block)):
+            by_rank.append((p, (p - 1) % current_block))
+        odd = jnp.zeros(
+            (*m.shape[:out_dim], current_block * outcome_arr, *m.shape[out_dim + 1 :]), m.dtype
+        )
+        odd = lax.dynamic_update_slice_in_dim(odd, m, val * outcome_arr, axis=out_dim)
+        tmp = reached = m
+        x_new = current_block // 2
+        for q in tuple(range(1, x_new + 1)):
+            tmp = jax.lax.ppermute(tmp, "shard", in_order)
+            odd = lax.dynamic_update_slice_in_dim(
+                odd, tmp, (val - q) % current_block * outcome_arr, axis=out_dim
+            )
+            if q < current_block - x_new:
+                reached = jax.lax.ppermute(reached, "shard", by_rank)
+                odd = lax.dynamic_update_slice_in_dim(
+                    odd, reached, (val + q) % current_block * outcome_arr, axis=out_dim
+                )
+        return odd
+
     whole = (
         lax.all_gather(w_qkv, "shard", axis=0, tiled=True),
         lax.all_gather(w_out, "shard", axis=0, tiled=True),
-        lax.all_gather(w_up, "shard", axis=0, tiled=True),
+        follow_ports(0, w_up),
         lax.all_gather(w_down, "shard", axis=0, tiled=True),
         lax.all_gather(vectors, "shard", axis=0, tiled=True),
     )

time: 1820 us -> 1940 us (1.066)
  waiting for transfers between devices: 1380 us -> 1440 us
  starting transfers between devices: 19.1 us -> 42.9 us
    ppermute x0 -> x7, waiting for transfers between devices: none -> 140 us  [the longest x4 112 us: follow_ports(): tmp = jax.lax.ppermute(tmp, 'shard', in_order)]
    all_gather x1, waiting for transfers between devices: 86.9 us -> 0.01 us  [per_device(): lax.all_gather(w_qkv, 'shard', axis=0, tiled=True)]
    unnamed x19, waiting for transfers between devices: 256 us -> 331 us
    all_gather x1, blocking collectives: 33.4 us -> 87.2 us  [per_device(): lax.all_gather(vectors, 'shard', axis=0, tiled=True)]
    unnamed x2, blocking collectives: 110 us -> 64.2 us
    all_gather x1, waiting for transfers between devices: 44.5 us -> 17.3 us  [per_device(): lax.all_gather(w_out, 'shard', axis=0, tiled=True)]
    all_gather x1, waiting for transfers between devices: 25.7 us -> 0.01 us  [per_device(): lax.all_gather(parted[3], 'rep', axis=0, tiled=True)]
    ppermute x0 -> x7, starting transfers between devices: none -> 19.6 us  [the longest x3 11 us: follow_ports(): reached = jax.lax.ppermute(reached, 'shard', by_rank)]
  transfers between devices with their start and end apart: 16 -> 23, of which waited for: 11 -> 14; matrix products, arithmetic and copies ran while one was open for 16% -> 14% of each run, Pallas kernels for 0% -> 0%
where the time goes in v1:
time: 1940 us; the launch traced here: 1930 us
  waiting for transfers between devices  1440 us (74%)
  blocking collectives  207 us (11%)
  matrix products  119 us (6%)
  local copies, waits for them, and re-layouts  97.4 us (5%)
  starting transfers between devices  42.9 us (2%)
    reduce_scatter x1, waiting for transfers between devices, per_device(): lax.psum_scatter(terms[2], 'shard', scatter_dimension=0, tiled=True)  335 us
    unnamed x19, waiting for transfers between devices  331 us
    reduce_scatter x1, waiting for transfers between devices, per_device(): lax.psum_scatter(terms[0], 'shard', scatter_dimension=0, tiled=True)  272 us
    all_gather x1, waiting for transfers between devices, per_device(): lax.all_gather(w_up, 'shard', axis=0, tiled=True)  141 us
    ppermute x4, waiting for transfers between devices, follow_ports(): tmp = jax.lax.ppermute(tmp, 'shard', in_order)  112 us
    all_gather x1, waiting for transfers between devices, per_device(): lax.all_gather(w_down, 'shard', axis=0, tiled=True)  101 us
    reduce_scatter x1, waiting for transfers between devices, per_device(): lax.psum_scatter(terms[1], 'shard', scatter_dimension=0, tiled=True)  101 us
    all_gather x1, blocking collectives, per_device(): lax.all_gather(vectors, 'shard', axis=0, tiled=True)  87.2 us
  transfers between devices with their start and end apart: 23, of which 14 were waited for; matrix products, arithmetic and copies ran while one was open for 14% of the time, Pallas kernels for 0%

profile of v1, /device:TPU:0, one launch (start us, length us, event | category | flops | bytes accessed | tf_op | source)
XLA Modules:
  0.0 1928.2 jit_solution(17755222769274136291)
XLA Ops:
  16.8 87.2 %all-gather = bf16[8,144,8]{1,2,0:T(8,128)(2,1)S(1)} all-gather(bf16[1,144,8]{1,2,0:T(8,128)(2,1)} %bitcast.145), channel_id=1, replica_groups=mesh['rep'=4,'shard'=8] {'shard'}, dimensions={0}, use_global_device_ids=true | all-gather | bytes 20736 | tf_op jit(solution)/shard_map/all_gather | solution.py:222
  116.3 68.4 %collective-permute-done.2 = bf16[144,4304]{1,0:T(8,128)(2,1)} collective-permute-done((bf16[144,4304]{1,0:T(8,128)(2,1)}, bf16[144,4304]{1,0:T(8,128)(2,1)}, u32[]{:S(2)}, u32[]{:S(2)}) %collective-permute-start.2) | collective-permute-done | bytes 1239584 | tf_op jit(solution)/shard_map/ppermute | solution.py:206
  200.1 31.7 %collective-permute-done.4 = bf16[144,4304]{1,0:T(8,128)(2,1)S(1)} collective-permute-done((bf16[144,4304]{1,0:T(8,128)(2,1)}, bf16[144,4304]{1,0:T(8,128)(2,1)S(1)}, u32[]{:S(2)}, u32[]{:S(2)}) %collective-permute-start.4) | collective-permute-done | bytes 1239584 | tf_op jit(solution)/shard_map/ppermute | solution.py:206
  236.8 26.1 %collective-permute-done.5 = bf16[144,4304]{1,0:T(8,128)(2,1)S(1)} collective-permute-done((bf16[144,4304]{1,0:T(8,128)(2,1)S(1)}, bf16[144,4304]{1,0:T(8,128)(2,1)S(1)}, u32[]{:S(2)}, u32[]{:S(2)}) %collective-permute-start.5) | collective-permute-done | bytes 1239584 | tf_op jit(solution)/shard_map/ppermute | solution.py:211
  264.0 11.8 collective-permute-done.6
  288.3 17.3 all-gather.16.cloned.1.call-done
  327.6 21.6 %copy.63 = f32[1152,4304]{1,0:T(8,128)} copy(f32[1152,4304]{0,1:T(8,128)} %convolution_bitcast_fusion) | data formatting | bytes 39665664
  349.9 101.4 %all-gather.18.cloned.1.call-done = bf16[1152,4304]{1,0:T(8,128)(2,1)} async-done(((bf16[144,4304]{1,0:T(8,128)(2,1)}), bf16[1152,4304]{1,0:T(8,128)(2,1)}) %all-gather.18.cloned.1.call-update) | async-done | bytes 9916432 | tf_op jit(solution)/shard_map/all_gather | solution.py:221
  451.2 11.4 fusion.98
  462.6 322.3 %reduce-scatter.24.cloned.1.call-done = f32[144,4304]{1,0:T(8,128)} async-done(((f32[1152,4304]{1,0:T(8,128)}), f32[144,4304]{1,0:T(8,128)}) %reduce-scatter.24.cloned.1.call-update) | async-done | bytes 2479120
  789.8 141.0 %all-gather.20.cloned.1.call-done = bf16[1152,4304]{1,0:T(8,128)(2,1)} async-done(((bf16[144,4304]{1,0:T(8,128)(2,1)}), bf16[1152,4304]{1,0:T(8,128)(2,1)}) %all-gather.20.cloned.1.call-update) | async-done | bytes 9916432 | tf_op jit(solution)/shard_map/all_gather | solution.py:228
  954.6 9.1 fusion.51
  963.6 9.6 fusion.93
  978.0 9.0 fusion.69
  987.7 11.5 fusion.65
  1027.8 100.7 %reduce-scatter.20.cloned.1.call-done = f32[144,1152]{1,0:T(8,128)} async-done(((f32[1152,1152]{1,0:T(8,128)}), f32[144,1152]{1,0:T(8,128)}) %reduce-scatter.20.cloned.1.call-update) | async-done | bytes 663568 | tf_op jit(solution)/shard_map/reduce_scatter | solution.py:238
  1128.6 271.9 %reduce-scatter.18.cloned.1.call-done = f32[144,3456]{1,0:T(8,128)} async-done(((f32[1152,3456]{1,0:T(8,128)}), f32[144,3456]{1,0:T(8,128)}) %reduce-scatter.18.cloned.1.call-update) | async-done | bytes 1990672 | tf_op jit(solution)/shard_map/reduce_scatter | solution.py:237
  1400.5 334.6 %reduce-scatter.22.cloned.1.call-done = f32[144,4304]{1,0:T(8,128)} async-done(((f32[1152,4304]{1,0:T(8,128)}), f32[144,4304]{1,0:T(8,128)}) %reduce-scatter.22.cloned.1.call-update) | async-done | bytes 2479120 | tf_op jit(solution)/shard_map/reduce_scatter | solution.py:239
  1735.1 58.0 %fusion.90 = (f32[48,3456]{1,0:T(8,128)}, f32[48,1152]{1,0:T(8,128)S(1)}, f32[40,4304]{1,0:T(8,128)}) fusion(f32[144,3456]{1,0:T(8,128)} %reduce-scatter.18.cloned.1.call-done, f32[144,1152]{1,0:T(8,128)} %reduce-scatter.20.cloned.1.call-done, f32[144,4304]{1,0:T(8,128)} %reduce-scatter.22.cloned.1.call-done), kind=kCustom, calls=%all-reduce-scatter.3 | all-reduce-scatter fusion | flops 1573378 | bytes 6707200
  1808.2 9.5 collective-permute-start.9
  1826.5 9.4 fusion.23
  1836.0 10.6 collective-permute-start.8
  1847.9 42.1 %psum.7 = f32[4304]{0:T(1024)} all-reduce(f32[4304]{0:T(1024)S(1)} %copy-done.33), channel_id=1, replica_groups=mesh['rep'=4,'shard'=8] {'rep','shard'}, use_global_device_ids=true, to_apply=%region_30.31 | all-reduce | flops 4304 | bytes 34432 | tf_op jit(solution)/shard_map/psum | solution.py:235
  1903.3 8.8 all-gather.2
  (202 shorter events, 186.8 us)
Async XLA Ops:
  7.2 269.8 %all-gather.14.cloned.1.call-start = ((), (), s32[]{:S(2)}) async-start(), calls=%async_computation.5 | async-start | bytes 8957952 | tf_op jit(solution)/shard_map/all_gather | solution.py:218
  7.9 297.7 %all-gather.16.cloned.1.call-start = ((), (), s32[]{:S(2)}) async-start(), calls=%async_computation.6 | async-start | bytes 2985984 | tf_op jit(solution)/shard_map/all_gather | solution.py:219
  8.7 442.6 %all-gather.18.cloned.1.call-start = ((), (), s32[]{:S(2)}) async-start(), calls=%async_computation.7 | async-start | bytes 11280384 | tf_op jit(solution)/shard_map/all_gather | solution.py:221
  9.4 775.5 %reduce-scatter.24.cloned.1.call-start = ((), (), s32[]{:S(2)}) async-start(), calls=%async_computation.15 | async-start | bytes 22560768
  9.4 94.7 %collective-permute-start = (bf16[144,4304]{1,0:T(8,128)(2,1)}, bf16[144,4304]{1,0:T(8,128)(2,1)}, u32[]{:S(2)}, u32[]{:S(2)}) collective-permute-start(bf16[144,4304]{1,0:T(8,128)(2,1)} %param.12), channel_id=1, source_target_pairs={{0,1},{1,2},{2,3},{3,4},{4,5},{5,6},{6,7},{7,0},{8,9},{9,10},{10,1... | collective-permute-start | bytes 3718664 | tf_op jit(solution)/shard_map/ppermute | solution.py:206
  12.5 98.0 %collective-permute-start.1 = (bf16[144,4304]{1,0:T(8,128)(2,1)}, bf16[144,4304]{1,0:T(8,128)(2,1)}, u32[]{:S(2)}, u32[]{:S(2)}) collective-permute-start(bf16[144,4304]{1,0:T(8,128)(2,1)} %param.12), channel_id=1, source_target_pairs={{0,7},{1,0},{2,1},{3,2},{4,3},{5,4},{6,5},{7,6},{8,15},{9,8},{10,9... | collective-permute-start | bytes 3718664 | tf_op jit(solution)/shard_map/ppermute | solution.py:211
  104.2 80.5 %collective-permute-start.2 = (bf16[144,4304]{1,0:T(8,128)(2,1)}, bf16[144,4304]{1,0:T(8,128)(2,1)}, u32[]{:S(2)}, u32[]{:S(2)}) collective-permute-start(bf16[144,4304]{1,0:T(8,128)(2,1)} %collective-permute-done), channel_id=1, source_target_pairs={{0,1},{1,2},{2,3},{3,4},{4,5},{5,6},{6,7},{7,0},{8,9},{9,10},{10,1... | collective-permute-start | bytes 3718664 | tf_op jit(solution)/shard_map/ppermute | solution.py:206
  110.5 83.7 %collective-permute-start.3 = (bf16[144,4304]{1,0:T(8,128)(2,1)}, bf16[144,4304]{1,0:T(8,128)(2,1)S(1)}, u32[]{:S(2)}, u32[]{:S(2)}) collective-permute-start(bf16[144,4304]{1,0:T(8,128)(2,1)} %collective-permute-done.1), channel_id=1, source_target_pairs={{0,7},{1,0},{2,1},{3,2},{4,3},{5,4},{6,5},{7,6},{8,15},{9,8},{10,9... | collective-permute-start | bytes 3718664 | tf_op jit(solution)/shard_map/ppermute | solution.py:211
  184.7 47.1 %collective-permute-start.4 = (bf16[144,4304]{1,0:T(8,128)(2,1)}, bf16[144,4304]{1,0:T(8,128)(2,1)S(1)}, u32[]{:S(2)}, u32[]{:S(2)}) collective-permute-start(bf16[144,4304]{1,0:T(8,128)(2,1)} %collective-permute-done.2), channel_id=1, source_target_pairs={{0,1},{1,2},{2,3},{3,4},{4,5},{5,6},{6,7},{7,0},{8,9},{9,10},{10,1... | collective-permute-start | bytes 3718664 | tf_op jit(solution)/shard_map/ppermute | solution.py:206
  194.2 68.7 %collective-permute-start.5 = (bf16[144,4304]{1,0:T(8,128)(2,1)S(1)}, bf16[144,4304]{1,0:T(8,128)(2,1)S(1)}, u32[]{:S(2)}, u32[]{:S(2)}) collective-permute-start(bf16[144,4304]{1,0:T(8,128)(2,1)S(1)} %collective-permute-done.3), channel_id=1, source_target_pairs={{0,7},{1,0},{2,1},{3,2},{4,3},{5,4},{6,5},{7,6},{8,15},{9,8},{10,9... | collective-permute-start | bytes 3718664 | tf_op jit(solution)/shard_map/ppermute | solution.py:211
  231.8 44.0 %collective-permute-start.6 = (bf16[144,4304]{1,0:T(8,128)(2,1)S(1)}, bf16[144,4304]{1,0:T(8,128)(2,1)S(1)}, u32[]{:S(2)}, u32[]{:S(2)}) collective-permute-start(bf16[144,4304]{1,0:T(8,128)(2,1)S(1)} %collective-permute-done.4), channel_id=1, source_target_pairs={{0,1},{1,2},{2,3},{3,4},{4,5},{5,6},{6,7},{7,0},{8,9},{9,10},{10,1... | collective-permute-start | bytes 3718664 | tf_op jit(solution)/shard_map/ppermute | solution.py:206
  308.5 622.3 %copy-start.23 = (f32[256]{0:T(256)}, f32[256]{0:T(256)S(1)}, u32[]{:S(2)}) copy-start(f32[256]{0:T(256)S(1)} %broadcast_multiply_fusion.4) | copy-start | bytes 3076
  349.2 581.5 %all-gather.20.cloned.1.call-start = ((), (), s32[]{:S(2)}) async-start(), calls=%async_computation.8 | async-start | bytes 11280384 | tf_op jit(solution)/shard_map/all_gather | solution.py:228
  349.8 670.6 %all-reduce.11.cloned.1.call-start = ((), (), s32[]{:S(2)}) async-start(), calls=%async_computation.17 | async-start | bytes 8814592
  789.7 338.8 %reduce-scatter.20.cloned.1.call-start = ((), (), s32[]{:S(2)}) async-start(), calls=%async_computation.10 | async-start | bytes 5971968 | tf_op jit(solution)/shard_map/reduce_scatter | solution.py:238
  944.5 455.9 %reduce-scatter.18.cloned.1.call-start = ((), (), s32[]{:S(2)}) async-start(), calls=%async_computation.9 | async-start | bytes 17915904 | tf_op jit(solution)/shard_map/reduce_scatter | solution.py:237
  987.0 748.1 %reduce-scatter.22.cloned.1.call-start = ((), (), s32[]{:S(2)}) async-start(), calls=%async_computation.11 | async-start | bytes 22560768 | tf_op jit(solution)/shard_map/reduce_scatter | solution.py:239
  999.2 890.7 %reduce-scatter.26.cloned.1.call-start = ((), (), s32[]{:S(2)}) async-start(), calls=%async_computation.16 | async-start | bytes 663552
  1014.8 898.2 %all-gather.26.cloned.1.call-start = ((), (), s32[]{:S(2)}) async-start(), calls=%async_computation.14 | async-start | bytes 3481600 | tf_op jit(solution)/shard_map/all_gather | solution.py:254
  1027.8 888.1 %all-gather.22.cloned.1.call-start = ((), (), s32[]{:S(2)}) async-start(), calls=%async_computation.12 | async-start | bytes 2764800 | tf_op jit(solution)/shard_map/all_gather | solution.py:251
  1795.0 3.2 collective-permute-start.7
  1807.2 111.4 %all-gather.24.cloned.1.call-start = ((), (), s32[]{:S(2)}) async-start(), calls=%async_computation.13 | async-start | bytes 3481600 | tf_op jit(solution)/shard_map/all_gather | solution.py:253
  1808.2 10.1 collective-permute-start.9
  1836.0 67.1 %collective-permute-start.8 = (f32[36,1152]{1,0:T(8,128)S(1)}, f32[36,1152]{1,0:T(8,128)S(1)}, u32[]{:S(2)}, u32[]{:S(2)}) collective-permute-start(f32[36,1152]{1,0:T(8,128)S(1)} %slice.59), channel_id=1, source_target_pairs={{0,8},{8,16},{16,24},{1,9},{9,17},{17,25},{2,10},{10,18},{18,26},{... | collective-permute-start | bytes 497672
  (38 other events, 1467.1 us)
Sparse Core Ops, SparseCore 0:
  10.2 218.1 all-gather.13
  230.5 75.0 all-gather.15
  307.8 143.3 all-gather.17
  455.0 329.7 reduce-scatter.23
  786.9 143.8 all-gather.19
  933.0 87.3 all-reduce.10
  1024.0 104.5 reduce-scatter.19
  1132.4 267.9 reduce-scatter.17
  1404.4 330.6 reduce-scatter.21
  1738.2 61.7 reduce-scatter.25
  1801.5 25.4 all-gather.25
  1828.5 26.1 all-gather.21
  1856.2 27.3 all-gather.23
